TPU v7x, 256 devices: a whole 4x4x8 slice. The times are simulated.
256 devices in a mesh: grid: 32 (over y, x, core), rows: 8 (over z).
Axes of the slice: x: 4, y: 4, z: 8, core: 2. Of those that a mesh axis runs over, the one named last changes fastest.
Arguments:
- density: bfloat16 [32, 128, 4096], P(None, 'rows', 'grid'), as said below
- basis_values: bfloat16 [64, 16, 128, 512], P('grid', None, 'rows'), may hold values from -0.59765625 to 0.59765625
- grid_points: float32 [64, 3, 512], P('grid'), may hold values from -4 to 4
- grid_weights: float32 [64, 512], P('grid'), may hold values from 0.05 to 1
- screened_blocks: int32 [64, 16], P('grid'), may hold values from 0 to 31, as said below
Outputs:
- exchange: float32 [32, 128, 4096], P(None, 'rows', 'grid')
Inputs may be any that keep to these rules, and one draw needn't show every extreme that they name: density is symmetric: density[a, i, b * 128 + j] equals density[b, j, a * 128 + i]. `screened_blocks`: each row holds 16 distinct block numbers.
All inputs are finite; a program needn't handle non-finite values.
Results may differ from a plain program's by a relative error of at most 0.00055.
The roundings to bfloat16 on the way count: a program that leaves them out, or rounds other values in their place, can miss the bound.
Values may be sent and summed in bfloat16 or wider, within the bound.
A program may use at most 64 MiB of HBM per device.

v0:
```python
import jax
import jax.numpy as jnp
from jax import lax
from jax.sharding import PartitionSpec as P


def copy_for_each(shard, axis):
    copies = jnp.broadcast_to(shard, (lax.axis_size(axis), *shard.shape))
    return lax.all_to_all(copies, axis, split_axis=0, concat_axis=0, tiled=True)


def joined_along(blocks, dim):
    shape = list(blocks.shape[1:])
    shape[dim] *= blocks.shape[0]
    return jnp.moveaxis(blocks, 0, dim).reshape(shape)


def gather_directly(shard, axis, dim):
    blocks = copy_for_each(shard, axis)
    return joined_along(blocks, dim)


def body(density, basis_values, grid_points, grid_weights, screened_blocks):
    nblocks = density.shape[0]
    rows_mine = density.shape[1]
    block_size = rows_mine * lax.axis_size("rows")
    nbasis = nblocks * block_size
    nsig = basis_values.shape[1]
    npoints = basis_values.shape[3]
    stripe = lax.all_gather(density, "grid", axis=2, tiled=True)
    totals = jnp.zeros((nblocks, rows_mine, nblocks, block_size), jnp.float32)
    for batch_index in range(basis_values.shape[0]):
        blocks = screened_blocks[batch_index]
        row_pick = jnp.take(stripe, blocks, axis=0).reshape(nsig * rows_mine, nblocks, block_size)
        chosen = jnp.take(row_pick, blocks, axis=1)
        local_values = basis_values[batch_index]
        x_mine = local_values.reshape(nsig * rows_mine, npoints)
        fsum = jnp.einsum(
            "mtk,tkp->mp",
            chosen,
            gather_directly(local_values, "rows", 1),
            preferred_element_type=jnp.float32,
        )
        fmat = fsum.astype(jnp.bfloat16)
        intersection_part = lax.dot_general(
            x_mine, fmat, (((0,), (0,)), ((), ())), preferred_element_type=jnp.float32
        )
        intersection = lax.psum(intersection_part, "rows")
        places = grid_points[batch_index]
        weights = grid_weights[batch_index]
        diffs = places[:, :, None] - places[:, None, :]
        kern = 1.0 / jnp.sqrt(jnp.sum(diffs * diffs, axis=0) + 0.5)
        mixed = (weights[:, None] * kern * intersection).astype(jnp.bfloat16)
        potential = (
            jnp.dot(x_mine, mixed, preferred_element_type=jnp.float32) * weights[None, :]
        ).astype(jnp.bfloat16)
        potential = potential.reshape(nsig, rows_mine, npoints)
        block_k = jnp.einsum(
            "mp,tkp->mtk",
            x_mine,
            lax.all_gather(potential, "rows", axis=1, tiled=True),
            preferred_element_type=jnp.float32,
        )
        block_k = block_k.reshape(nsig, rows_mine, nsig, block_size)
        totals = totals.at[blocks[:, None], :, blocks[None, :], :].add(
            block_k.transpose(0, 2, 1, 3)
        )
    return lax.psum_scatter(
        totals.reshape(nblocks, rows_mine, nbasis), "grid", scatter_dimension=2, tiled=True
    )


def solution(mesh):
    placed = (
        P(None, "rows", "grid"),
        P("grid", None, "rows", None),
        P("grid", None, None),
        P("grid", None),
        P("grid", None),
    )
    return jax.shard_map(
        body, mesh=mesh, in_specs=placed, out_specs=P(None, "rows", "grid"), check_vma=False
    )
```

profile of v0, /device:TPU:2, one launch (start us, length us, event | category | flops | bytes accessed | tf_op | source)
XLA Modules:
  0.0 494.6 jit_solution(1196830963108560420)
XLA Ops:
  8.6 59.6 %all_to_all.10 = bf16[8,16,16,512]{3,2,1,0:T(8,128)(2,1)} all-to-all(bf16[8,16,16,512]{3,2,1,0:T(8,128)(2,1)S(1)} %broadcast_in_dim.59), channel_id=1, replica_groups=mesh['grid'=32,'rows'=8] {'rows'}, dimensions={0} | all-to-all | bytes 4194304 | tf_op jit(solution)/shard_map/all_to_all | solution.py:9
  69.8 3.7 all-to-all-start
  73.7 3.2 copy.34
  76.8 46.5 %all-to-all-done = bf16[8,16,16,512]{3,2,1,0:T(8,128)(2,1)S(1)} async-done(((bf16[8,16,16,512]{3,2,1,0:T(8,128)(2,1)}), bf16[8,16,16,512]{3,2,1,0:T(8,128)(2,1)S(1)}, u32[]{:S(2)}, u32[]{:S(2)}) %all-to-all-start) | async-done | bytes 2097184 | tf_op jit(solution)/shard_map/all_to_all | solution.py:9
  124.9 2.9 gather_fusion.2
  131.1 2.9 gather_fusion
  137.2 4.1 convolution_bitcast_fusion.2
  141.3 3.3 convolution_bitcast_fusion.3
  146.0 77.3 %all-reduce.3.cloned.1.call-done = (f32[512,512]{0,1:T(8,128)}, f32[512,512]{0,1:T(8,128)}) async-done(((f32[512,512]{0,1:T(8,128)}, f32[512,512]{0,1:T(8,128)}), (f32[512,512]{0,1:T(8,128)}, f32[512,512]{0,1:T(8,128)})) %all-reduce.3.cloned.1.call-update) | async-done | bytes 2097168 | tf_op jit(solution)/shard_map/psum | solution.py:48
  223.3 2.3 fusion
  226.4 2.3 fusion.1
  229.3 36.4 %all-gather.6.cloned.1.call-done = bf16[16,128,512]{2,1,0:T(8,128)(2,1)} async-done(((bf16[16,16,512]{2,1,0:T(8,128)(2,1)}), bf16[16,128,512]{2,1,0:T(8,128)(2,1)}) %all-gather.6.cloned.1.call-update) | async-done | bytes 2097168 | tf_op jit(solution)/shard_map/all_gather | solution.py:61
  265.7 2.3 convolution_bitcast_fusion.1
  268.0 2.0 copy.30
  270.0 2.3 copy.31
  272.2 34.5 %all-gather.8.cloned.1.call-done = bf16[16,128,512]{2,1,0:T(8,128)(2,1)} async-done(((bf16[16,16,512]{2,1,0:T(8,128)(2,1)}), bf16[16,128,512]{2,1,0:T(8,128)(2,1)}) %all-gather.8.cloned.1.call-update) | async-done | bytes 2097168 | tf_op jit(solution)/shard_map/all_gather | solution.py:61
  306.8 3.6 convolution_bitcast_fusion
  310.4 3.1 copy.35
  313.5 3.6 copy.36
  317.1 4.2 broadcast_in_dim.51
  321.3 28.4 %scatter_fusion = f32[32,16,32,128]{3,1,2,0:T(8,128)} fusion(f32[32,16,32,128]{3,1,2,0:T(8,128)} %broadcast_in_dim.51, s32[256]{0:T(256)S(1)} %reshape.140, f32[256,16,128]{2,1,0:T(8,128)S(1)} %bitcast.107), kind=kCustom, calls=%fused_computation.4 | custom fusion | flops 524288 | bytes 6293504 | tf_op jit(solution)/shard_map/scatter-add | solution.py:65
  349.7 31.8 %scatter_fusion.1 = f32[32,16,32,128]{3,1,2,0:T(8,128)} fusion(f32[32,16,32,128]{3,1,2,0:T(8,128)} %scatter_fusion, s32[256]{0:T(256)S(1)} %reshape.146, f32[256,16,128]{2,1,0:T(8,128)} %bitcast.108), kind=kCustom, calls=%fused_computation.5 | custom fusion | flops 524288 | bytes 6293504 | tf_op jit(solution)/shard_map/scatter-add | solution.py:65
  381.5 7.8 %copy_bitcast_fusion = f32[32,16,4096]{2,1,0:T(8,128)} fusion(f32[32,16,32,128]{3,1,2,0:T(8,128)} %scatter_fusion.1), kind=kLoop, calls=%fused_computation.6 | loop fusion | bytes 16777216 | tf_op jit(solution)/shard_map/reshape | solution.py:69
  389.3 98.8 %reduce-scatter.2.cloned.1.call-done = f32[32,16,128]{2,1,0:T(8,128)} async-done(((f32[32,16,4096]{2,1,0:T(8,128)}), f32[32,16,128]{2,1,0:T(8,128)}) %reduce-scatter.2.cloned.1.call-update) | async-done | bytes 262160 | tf_op jit(solution)/shard_map/reduce_scatter | solution.py:68
  (49 shorter events, 14.5 us)
Async XLA Ops:
  6.5 118.4 %all-gather.4.cloned.1.call-start = ((), (), s32[]{:S(2)}) async-start(), calls=%async_computation.3 | async-start | bytes 4325376 | tf_op jit(solution)/shard_map/all_gather | solution.py:30
  69.8 3.8 copy-start.3
  69.8 53.5 %all-to-all-start = ((bf16[8,16,16,512]{3,2,1,0:T(8,128)(2,1)}), bf16[8,16,16,512]{3,2,1,0:T(8,128)(2,1)S(1)}, u32[]{:S(2)}, u32[]{:S(2)}) async-start(bf16[8,16,16,512]{3,2,1,0:T(8,128)(2,1)} %broadcast_in_dim.55), calls=%async_computation | async-start | bytes 4194304 | tf_op jit(solution)/shard_map/all_to_all | solution.py:9
  73.5 149.8 %all-reduce.3.cloned.1.call-start = ((), (), s32[]{:S(2)}) async-start(), calls=%async_computation.7 | async-start | bytes 4194304 | tf_op jit(solution)/shard_map/psum | solution.py:48
  137.2 4.1 copy-start
  144.6 0.7 copy-start.1
  144.6 1.4 copy-start.2
  144.6 121.1 %all-gather.6.cloned.1.call-start = ((), (), s32[]{:S(2)}) async-start(), calls=%async_computation.4 | async-start | bytes 2359296 | tf_op jit(solution)/shard_map/all_gather | solution.py:61
  225.7 81.1 %all-gather.8.cloned.1.call-start = ((), (), s32[]{:S(2)}) async-start(), calls=%async_computation.5 | async-start | bytes 2359296 | tf_op jit(solution)/shard_map/all_gather | solution.py:61
  228.7 259.3 %reduce-scatter.2.cloned.1.call-start = ((), (), s32[]{:S(2)}) async-start(), calls=%async_computation.6 | async-start | bytes 8650752 | tf_op jit(solution)/shard_map/reduce_scatter | solution.py:68
Sparse Core Ops, SparseCore 0:
  9.8 56.2 all-gather.3
  144.7 78.5 all-reduce.2
  225.8 39.8 all-gather.5
  267.3 39.4 all-gather.7
  389.4 98.5 reduce-scatter.1
where the time goes:
time: 496 us; the launch traced here: 495 us
  waiting for transfers between devices  294 us (59%)
  other arithmetic  61.6 us (12%)
  blocking collectives  59.6 us (12%)
  local copies, waits for them, and re-layouts  43.8 us (9%)
  matrix products  17.9 us (4%)
  between operations  13.4 us (3%)
    reduce_scatter x1, waiting for transfers between devices, body(): lax.psum_scatter(totals.reshape(nblocks, rows_mine, nbasis), 'grid', scat...  98.8 us
    psum x1, waiting for transfers between devices, body(): intersection = lax.psum(intersection_part, 'rows')  77.3 us
    all_gather x2, waiting for transfers between devices, body(): lax.all_gather(potential, 'rows', axis=1, tiled=True)  70.9 us
    scatter-add x2, other arithmetic, body(): totals.at[blocks[:, None], :, blocks[None, :], :]  60.2 us
    all_to_all x1, blocking collectives, copy_for_each(): return lax.all_to_all(copies, axis, split_axis=0, concat_axis=0, tiled=True)  59.6 us
    all_to_all x1, waiting for transfers between devices, copy_for_each(): return lax.all_to_all(copies, axis, split_axis=0, concat_axis=0, tiled=True)  46.5 us
  transfers between devices with their start and end apart: 6, of which 5 were waited for; matrix products, arithmetic and copies ran while one was open for 4% of the time, Pallas kernels for 0%

commit v1 on v0

--- a/solution.py
+++ b/solution.py
@@ -45,7 +45,11 @@
         intersection_part = lax.dot_general(
             x_mine, fmat, (((0,), (0,)), ((), ())), preferred_element_type=jnp.float32
         )
-        intersection = lax.psum(intersection_part, "rows")
+        intersection = intersection_part
+        for hop in (1, 2, 4):
+            intersection = intersection + lax.ppermute(
+                intersection, "rows", [(dev, dev ^ hop) for dev in range(8)]
+            )
         places = grid_points[batch_index]
         weights = grid_weights[batch_index]
         diffs = places[:, :, None] - places[:, None, :]

time: 496 us -> 618 us (1.25)
  waiting for transfers between devices: 294 us -> 385 us
  starting transfers between devices: 4.08 us -> 24.6 us
    ppermute x0 -> x6, waiting for transfers between devices: none -> 253 us  [body(): lax.ppermute(intersection, 'rows', [(dev, dev ^ hop) for dev in range(8)])]
    psum x1 -> x0, waiting for transfers between devices: 77.3 us -> none  [body(): intersection = lax.psum(intersection_part, 'rows')]
    all_to_all x1, waiting for transfers between devices: 46.5 us -> 0.01 us  [copy_for_each(): return lax.all_to_all(copies, axis, split_axis=0, concat_axis=0, tiled=True)]
    all_gather x2, waiting for transfers between devices: 70.9 us -> 32.4 us  [body(): lax.all_gather(potential, 'rows', axis=1, tiled=True)]
    ppermute x0 -> x6, starting transfers between devices: none -> 20.7 us  [body(): lax.ppermute(intersection, 'rows', [(dev, dev ^ hop) for dev in range(8)])]
  transfers between devices with their start and end apart: 6 -> 11, of which waited for: 5 -> 8; matrix products, arithmetic and copies ran while one was open for 4% -> 8% of each run, Pallas kernels for 0% -> 0%
where the time goes in v1:
time: 618 us; the launch traced here: 616 us
  waiting for transfers between devices  385 us (62%)
  other arithmetic  66.4 us (11%)
  blocking collectives  59.6 us (10%)
  local copies, waits for them, and re-layouts  49.9 us (8%)
  starting transfers between devices  24.6 us (4%)
  matrix products  17.4 us (3%)
  between operations  13.4 us (2%)
    ppermute x6, waiting for transfers between devices, body(): lax.ppermute(intersection, 'rows', [(dev, dev ^ hop) for dev in range(8)])  253 us
    reduce_scatter x1, waiting for transfers between devices, body(): lax.psum_scatter(totals.reshape(nblocks, rows_mine, nbasis), 'grid', scat...  98.7 us
    scatter-add x2, other arithmetic, body(): totals.at[blocks[:, None], :, blocks[None, :], :]  60.2 us
    all_to_all x1, blocking collectives, copy_for_each(): return lax.all_to_all(copies, axis, split_axis=0, concat_axis=0, tiled=True)  59.6 us
    all_gather x2, waiting for transfers between devices, body(): lax.all_gather(potential, 'rows', axis=1, tiled=True)  32.4 us
    ppermute x6, starting transfers between devices, body(): lax.ppermute(intersection, 'rows', [(dev, dev ^ hop) for dev in range(8)])  20.7 us
  transfers between devices with their start and end apart: 11, of which 8 were waited for; matrix products, arithmetic and copies ran while one was open for 8% of the time, Pallas kernels for 0%

profile of v1, /device:TPU:2, one launch (start us, length us, event | category | flops | bytes accessed | tf_op | source)
XLA Modules:
  0.0 616.1 jit_solution(948850153555150799)
XLA Ops:
  8.7 59.6 %all_to_all.10 = bf16[8,16,16,512]{3,2,1,0:T(8,128)(2,1)} all-to-all(bf16[8,16,16,512]{3,2,1,0:T(8,128)(2,1)S(1)} %broadcast_in_dim.59), channel_id=1, replica_groups=mesh['grid'=32,'rows'=8] {'rows'}, dimensions={0} | all-to-all | bytes 4194304 | tf_op jit(solution)/shard_map/all_to_all | solution.py:9
  69.9 3.7 all-to-all-start
  73.7 3.2 copy.34
  76.9 4.3 gather_fusion.2
  85.7 3.2 gather_fusion.3
  89.0 4.0 convolution_bitcast_fusion.2
  94.9 47.0 %collective-permute-done.3 = f32[512,512]{0,1:T(8,128)S(1)} collective-permute-done((f32[512,512]{0,1:T(8,128)}, f32[512,512]{0,1:T(8,128)S(1)}, u32[]{:S(2)}, u32[]{:S(2)}) %collective-permute-start.3) | collective-permute-done | bytes 1048608 | tf_op jit(solution)/shard_map/ppermute | solution.py:50
  147.3 41.9 %collective-permute-done.4 = f32[512,512]{0,1:T(8,128)S(1)} collective-permute-done((f32[512,512]{0,1:T(8,128)S(1)}, f32[512,512]{0,1:T(8,128)S(1)}, u32[]{:S(2)}, u32[]{:S(2)}) %collective-permute-start.4) | collective-permute-done | bytes 1048608 | tf_op jit(solution)/shard_map/ppermute | solution.py:50
  189.4 6.3 %collective-permute-start.5 = (f32[512,512]{0,1:T(8,128)S(1)}, f32[512,512]{0,1:T(8,128)}, u32[]{:S(2)}, u32[]{:S(2)}) collective-permute-start(f32[512,512]{0,1:T(8,128)S(1)} %add.68), channel_id=1, source_target_pairs={{0,4},{1,5},{2,6},{3,7},{4,0},{5,1},{6,2},{7,3},{8,12},{9,13},{10,... | collective-permute-start | bytes 3145736 | tf_op jit(solution)/shard_map/ppermute | solution.py:50
  206.1 34.3 %collective-permute-done.5 = f32[512,512]{0,1:T(8,128)} collective-permute-done((f32[512,512]{0,1:T(8,128)S(1)}, f32[512,512]{0,1:T(8,128)}, u32[]{:S(2)}, u32[]{:S(2)}) %collective-permute-start.5) | collective-permute-done | bytes 1048608 | tf_op jit(solution)/shard_map/ppermute | solution.py:50
  245.6 37.7 %collective-permute-done = f32[512,512]{0,1:T(8,128)S(1)} collective-permute-done((f32[512,512]{0,1:T(8,128)S(1)}, f32[512,512]{0,1:T(8,128)S(1)}, u32[]{:S(2)}, u32[]{:S(2)}) %collective-permute-start) | collective-permute-done | bytes 1048608 | tf_op jit(solution)/shard_map/ppermute | solution.py:50
  283.5 6.1 collective-permute-start.1
  289.6 46.1 %collective-permute-done.1 = f32[512,512]{0,1:T(8,128)S(1)} collective-permute-done((f32[512,512]{0,1:T(8,128)S(1)}, f32[512,512]{0,1:T(8,128)S(1)}, u32[]{:S(2)}, u32[]{:S(2)}) %collective-permute-start.1) | collective-permute-done | bytes 1048608 | tf_op jit(solution)/shard_map/ppermute | solution.py:50
  335.9 3.9 collective-permute-start.2
  340.5 46.0 %collective-permute-done.2 = f32[512,512]{0,1:T(8,128)} collective-permute-done((f32[512,512]{0,1:T(8,128)S(1)}, f32[512,512]{0,1:T(8,128)}, u32[]{:S(2)}, u32[]{:S(2)}) %collective-permute-start.2) | collective-permute-done | bytes 1048608 | tf_op jit(solution)/shard_map/ppermute | solution.py:50
  395.9 32.4 %all-gather.6.cloned.1.call-done = bf16[16,128,512]{2,1,0:T(8,128)(2,1)} async-done(((bf16[16,16,512]{2,1,0:T(8,128)(2,1)}), bf16[16,128,512]{2,1,0:T(8,128)(2,1)}) %all-gather.6.cloned.1.call-update) | async-done | bytes 2097168 | tf_op jit(solution)/shard_map/all_gather | solution.py:65
  428.3 3.7 convolution_bitcast_fusion.1
  431.9 3.1 copy.30
  435.0 3.6 copy.31
  438.6 4.2 broadcast_in_dim.51
  442.8 31.8 %scatter_fusion = f32[32,16,32,128]{3,1,2,0:T(8,128)} fusion(f32[32,16,32,128]{3,1,2,0:T(8,128)} %broadcast_in_dim.51, s32[256]{0:T(256)S(1)} %reshape.140, f32[256,16,128]{2,1,0:T(8,128)} %bitcast.108), kind=kCustom, calls=%fused_computation.4 | custom fusion | flops 524288 | bytes 6293504 | tf_op jit(solution)/shard_map/scatter-add | solution.py:69
  474.7 28.4 %scatter_fusion.1 = f32[32,16,32,128]{3,1,2,0:T(8,128)} fusion(f32[32,16,32,128]{3,1,2,0:T(8,128)} %scatter_fusion, s32[256]{0:T(256)S(1)} %reshape.146, f32[256,16,128]{2,1,0:T(8,128)S(1)} %bitcast.107), kind=kCustom, calls=%fused_computation.5 | custom fusion | flops 524288 | bytes 6293504 | tf_op jit(solution)/shard_map/scatter-add | solution.py:69
  503.1 7.8 %copy_bitcast_fusion = f32[32,16,4096]{2,1,0:T(8,128)} fusion(f32[32,16,32,128]{3,1,2,0:T(8,128)} %scatter_fusion.1), kind=kLoop, calls=%fused_computation.6 | loop fusion | bytes 16777216 | tf_op jit(solution)/shard_map/reshape | solution.py:73
  510.9 98.7 %reduce-scatter.2.cloned.1.call-done = f32[32,16,128]{2,1,0:T(8,128)} async-done(((f32[32,16,4096]{2,1,0:T(8,128)}), f32[32,16,128]{2,1,0:T(8,128)}) %reduce-scatter.2.cloned.1.call-update) | async-done | bytes 262160 | tf_op jit(solution)/shard_map/reduce_scatter | solution.py:72
  (65 shorter events, 41.7 us)
Async XLA Ops:
  6.5 70.4 %all-gather.4.cloned.1.call-start = ((), (), s32[]{:S(2)}) async-start(), calls=%async_computation.3 | async-start | bytes 4325376 | tf_op jit(solution)/shard_map/all_gather | solution.py:30
  8.4 80.5 %copy-start = (bf16[1,16,16,512]{3,2,1,0:T(8,128)(2,1)}, bf16[1,16,16,512]{3,2,1,0:T(8,128)(2,1)S(1)}, u32[]{:S(2)}) copy-start(bf16[1,16,16,512]{3,2,1,0:T(8,128)(2,1)S(1)} %get-tuple-element.13) | copy-start | bytes 786436
  69.9 3.8 copy-start.5
  69.9 128.5 %all-to-all-start = ((bf16[8,16,16,512]{3,2,1,0:T(8,128)(2,1)}), bf16[8,16,16,512]{3,2,1,0:T(8,128)(2,1)S(1)}, u32[]{:S(2)}, u32[]{:S(2)}) async-start(bf16[8,16,16,512]{3,2,1,0:T(8,128)(2,1)} %broadcast_in_dim.55), calls=%async_computation | async-start | bytes 4194304 | tf_op jit(solution)/shard_map/all_to_all | solution.py:9
  73.6 315.7 %all-gather.8.cloned.1.call-start = ((), (), s32[]{:S(2)}) async-start(), calls=%async_computation.5 | async-start | bytes 2359296 | tf_op jit(solution)/shard_map/all_gather | solution.py:65
  93.0 52.8 %copy-start.3 = (f32[2,3,512]{2,0,1:T(2,128)S(1)}, f32[2,3,512]{2,0,1:T(2,128)}, u32[]{:S(2)}) copy-start(f32[2,3,512]{2,0,1:T(2,128)} %param.11) | copy-start | bytes 36868
  93.0 54.3 %copy-start.4 = (f32[2,512]{1,0:T(2,128)S(1)}, f32[2,512]{1,0:T(2,128)}, u32[]{:S(2)}) copy-start(f32[2,512]{1,0:T(2,128)} %param.12) | copy-start | bytes 12292
  93.0 48.9 %collective-permute-start.3 = (f32[512,512]{0,1:T(8,128)}, f32[512,512]{0,1:T(8,128)S(1)}, u32[]{:S(2)}, u32[]{:S(2)}) collective-permute-start(f32[512,512]{0,1:T(8,128)} %convolution_bitcast_fusion.2), channel_id=1, source_target_pairs={{0,1},{1,0},{2,3},{3,2},{4,5},{5,4},{6,7},{7,6},{8,9},{9,8},{10,11... | collective-permute-start | bytes 3145736 | tf_op jit(solution)/shard_map/ppermute | solution.py:50
  143.3 45.9 %collective-permute-start.4 = (f32[512,512]{0,1:T(8,128)S(1)}, f32[512,512]{0,1:T(8,128)S(1)}, u32[]{:S(2)}, u32[]{:S(2)}) collective-permute-start(f32[512,512]{0,1:T(8,128)S(1)} %add.67), channel_id=1, source_target_pairs={{0,2},{1,3},{2,0},{3,1},{4,6},{5,7},{6,4},{7,5},{8,10},{9,11},{10,... | collective-permute-start | bytes 3145736 | tf_op jit(solution)/shard_map/ppermute | solution.py:50
  189.4 50.9 %collective-permute-start.5 = (f32[512,512]{0,1:T(8,128)S(1)}, f32[512,512]{0,1:T(8,128)}, u32[]{:S(2)}, u32[]{:S(2)}) collective-permute-start(f32[512,512]{0,1:T(8,128)S(1)} %add.68), channel_id=1, source_target_pairs={{0,4},{1,5},{2,6},{3,7},{4,0},{5,1},{6,2},{7,3},{8,12},{9,13},{10,... | collective-permute-start | bytes 3145736 | tf_op jit(solution)/shard_map/ppermute | solution.py:50
  206.1 37.1 %copy-start.2 = (bf16[8,16,16,512]{3,2,0,1:T(8,128)(2,1)S(1)}, bf16[8,16,16,512]{3,2,0,1:T(8,128)(2,1)}, u32[]{:S(2)}) copy-start(bf16[8,16,16,512]{3,2,0,1:T(8,128)(2,1)} %copy.29) | copy-start | bytes 6291460
  243.1 185.1 %all-gather.6.cloned.1.call-start = ((), (), s32[]{:S(2)}) async-start(), calls=%async_computation.4 | async-start | bytes 2359296 | tf_op jit(solution)/shard_map/all_gather | solution.py:65
  245.5 37.8 %collective-permute-start = (f32[512,512]{0,1:T(8,128)S(1)}, f32[512,512]{0,1:T(8,128)S(1)}, u32[]{:S(2)}, u32[]{:S(2)}) collective-permute-start(f32[512,512]{0,1:T(8,128)S(1)} %convolution_bitcast_fusion.3), channel_id=1, source_target_pairs={{0,1},{1,0},{2,3},{3,2},{4,5},{5,4},{6,7},{7,6},{8,9},{9,8},{10,11... | collective-permute-start | bytes 3145736 | tf_op jit(solution)/shard_map/ppermute | solution.py:50
  283.5 52.2 %collective-permute-start.1 = (f32[512,512]{0,1:T(8,128)S(1)}, f32[512,512]{0,1:T(8,128)S(1)}, u32[]{:S(2)}, u32[]{:S(2)}) collective-permute-start(f32[512,512]{0,1:T(8,128)S(1)} %add.61), channel_id=1, source_target_pairs={{0,2},{1,3},{2,0},{3,1},{4,6},{5,7},{6,4},{7,5},{8,10},{9,11},{10,... | collective-permute-start | bytes 3145736 | tf_op jit(solution)/shard_map/ppermute | solution.py:50
  335.9 50.6 %collective-permute-start.2 = (f32[512,512]{0,1:T(8,128)S(1)}, f32[512,512]{0,1:T(8,128)}, u32[]{:S(2)}, u32[]{:S(2)}) collective-permute-start(f32[512,512]{0,1:T(8,128)S(1)} %add.62), channel_id=1, source_target_pairs={{0,4},{1,5},{2,6},{3,7},{4,0},{5,1},{6,2},{7,3},{8,12},{9,13},{10,... | collective-permute-start | bytes 3145736 | tf_op jit(solution)/shard_map/ppermute | solution.py:50
  340.5 48.8 %copy-start.1 = (bf16[1,16,16,512]{3,2,1,0:T(8,128)(2,1)S(1)}, bf16[1,16,16,512]{3,2,1,0:T(8,128)(2,1)}, u32[]{:S(2)}) copy-start(bf16[1,16,16,512]{3,2,1,0:T(8,128)(2,1)} %copy-done) | copy-start | bytes 786436
  388.9 220.6 %reduce-scatter.2.cloned.1.call-start = ((), (), s32[]{:S(2)}) async-start(), calls=%async_computation.6 | async-start | bytes 8650752 | tf_op jit(solution)/shard_map/reduce_scatter | solution.py:72
Sparse Core Ops, SparseCore 0:
  9.8 56.2 all-gather.3
  243.2 50.5 all-gather.7
  389.0 39.1 all-gather.5
  511.0 98.5 reduce-scatter.1
